TPU v7x, 32 devices: a whole 2x2x4 slice. The times are simulated.
32 devices in a mesh: dp: 2 (over x), row: 4 (over y, core), col: 4 (over z).
Axes of the slice: x: 2, y: 2, z: 4, core: 2. Of those that a mesh axis runs over, the one named last changes fastest.
Arguments:
- latents: float32 [24, 32, 128], P(('dp', 'row')), may hold values from -6 to 6
- labels: int32 [24], P(('dp', 'row')), may hold values from 0 to 999
- step_index: int32 [24], P(('dp', 'row')), may hold values from 1 to 8
- seeds: int32 [24], P(('dp', 'row')), may hold values from 0 to 2147483646
- class_table: bfloat16 [1000, 1152], replicated, may hold values from -6 to 6
- teacher_patch: bfloat16 [16, 1152], replicated, may hold values from -1.5 to 1.5
- teacher_mod: bfloat16 [1152, 3, 1152], P(('dp', 'row'), None, 'col'), may hold values from -0.1875 to 0.1875
- teacher_up: bfloat16 [1152, 4608], P(('dp', 'row'), 'col'), may hold values from -0.1875 to 0.1875
- teacher_down: bfloat16 [1152, 4608], P(('dp', 'row'), 'col'), may hold values from -0.09375 to 0.09375
- teacher_out: bfloat16 [16, 1152], replicated, may hold values from -0.1875 to 0.1875
- student_patch: bfloat16 [16, 1152], replicated, may hold values from -1.5 to 1.5
- student_mod: bfloat16 [1152, 3, 1152], P(('dp', 'row'), None, 'col'), may hold values from -0.1875 to 0.1875
- student_up: bfloat16 [1152, 4608], P(('dp', 'row'), 'col'), may hold values from -0.1875 to 0.1875
- student_down: bfloat16 [1152, 4608], P(('dp', 'row'), 'col'), may hold values from -0.09375 to 0.09375
- student_out: bfloat16 [16, 1152], replicated, may hold values from -0.1875 to 0.1875
Outputs:
- up_gradient: float32 [1152, 4608], P(('dp', 'row'), 'col')
- down_gradient: float32 [1152, 4608], P(('dp', 'row'), 'col')
All inputs are finite; a program needn't handle non-finite values.
Results may differ from a plain program's by a relative error of at most 0.002.
Values may be sent and summed in bfloat16 or wider, within the bound.
No kernel may reach another device: no remote copies, remote signals or barrier semaphores. Data moves between devices by JAX's collectives and lax.ppermute only.
A program may use at most 128 MiB of HBM per device.

v0:
```python
import math
import jax
import jax.numpy as jnp
from jax import lax
from jax.sharding import PartitionSpec as P

D = 1152
CLASSES = 1000
SEQ = 256
PATCH = 16
STEPS = 8
HALF_PI = 0.5 * math.pi
ROOT_TWO_PI = math.sqrt(2.0 / math.pi)


def plan(times):
    return (jnp.cos(HALF_PI * times), jnp.sin(HALF_PI * times))


def mixing(value):
    amount = jnp.int32(16)
    value = value ^ lax.shift_right_logical(value, amount)
    value = value * 73244475
    value = value ^ lax.shift_right_logical(value, amount)
    value = value * 73244475
    value = value ^ lax.shift_right_logical(value, amount)
    return value


def noise_of(seeds):
    total = SEQ * PATCH
    places = jnp.arange(total, dtype=jnp.int32).reshape(1, total // 128, 128)
    mixed = mixing(seeds[:, None, None] * 1103515245 + places * 40503 + 12345)
    uniform = (lax.shift_right_logical(mixed, jnp.int32(8)).astype(jnp.float32) + 0.5) * (
        1.0 / 16777216.0
    )
    return math.sqrt(2.0) * lax.erf_inv(2.0 * uniform - 1.0)


def time_features(times):
    half = D // 2
    freqs = jnp.exp(-math.log(10000.0) * jnp.arange(half, dtype=jnp.float32) / half)
    angle = (1000.0 * times)[:, None] * freqs[None, :]
    return jnp.concatenate([jnp.cos(angle), jnp.sin(angle)], axis=1)


def condition(times, labels, class_table):
    onehot = (labels[:, None] == jnp.arange(CLASSES, dtype=jnp.int32)[None, :]).astype(jnp.bfloat16)
    embedded = jnp.dot(onehot, class_table, preferred_element_type=jnp.float32)
    return jax.nn.silu(embedded + time_features(times)).astype(jnp.bfloat16)


def positions():
    quarter = D // 4
    omega = 1.0 / 10000.0 ** (jnp.arange(quarter, dtype=jnp.float32) / quarter)
    side = math.isqrt(SEQ)
    cells = jnp.arange(SEQ, dtype=jnp.int32)
    grid_row = (cells // side).astype(jnp.float32)
    grid_col = (cells % side).astype(jnp.float32)
    row_angle = grid_row[:, None] * omega[None, :]
    col_angle = grid_col[:, None] * omega[None, :]
    return jnp.concatenate(
        [jnp.sin(row_angle), jnp.cos(row_angle), jnp.sin(col_angle), jnp.cos(col_angle)], axis=1
    )


def layer_norm(values):
    center = values - jnp.mean(values, axis=-1, keepdims=True)
    spread = jnp.mean(center * center, axis=-1, keepdims=True)
    reciprocal = lax.rsqrt(spread + 1e-06)
    return (center * reciprocal, reciprocal)


def gelu_slope(pre):
    inner = ROOT_TWO_PI * (pre + 0.044715 * pre * pre * pre)
    tangent = jnp.tanh(inner)
    return 0.5 * (1.0 + tangent) + 0.5 * pre * (1.0 - tangent * tangent) * ROOT_TWO_PI * (
        1.0 + 3.0 * 0.044715 * pre * pre
    )


def contract_last(left, right):
    return lax.dot_general(
        left, right, (((1,), (1,)), ((), ())), preferred_element_type=jnp.float32
    )


def contract_first(left, right):
    return lax.dot_general(
        left, right, (((0,), (0,)), ((), ())), preferred_element_type=jnp.float32
    )


def network(state, mods, patch_weight, out_weight, pos, up_product, down_product):
    samples = state.shape[0]
    tokens = state.reshape(samples * SEQ, PATCH).astype(jnp.bfloat16)
    base = (
        jnp.dot(tokens, patch_weight, preferred_element_type=jnp.float32).reshape(samples, SEQ, D)
        + pos[None]
    )
    shift = mods[:, 0][:, None, :]
    scale = mods[:, 1][:, None, :]
    gate = mods[:, 2][:, None, :]
    normed, _ = layer_norm(base)
    act = (normed * (1.0 + scale) + shift).astype(jnp.bfloat16).reshape(samples * SEQ, D)
    pre = up_product(act)
    hidden = jax.nn.gelu(pre, approximate=True).astype(jnp.bfloat16)
    partial_out = down_product(hidden).astype(jnp.bfloat16)
    mixed = lax.psum(partial_out, "col").astype(jnp.float32)
    later = base + gate * mixed.reshape(samples, SEQ, D)
    final, reciprocal = layer_norm(later)
    velocity = contract_last(final.astype(jnp.bfloat16).reshape(samples * SEQ, D), out_weight)
    return (
        velocity.reshape(samples, SEQ * PATCH // 128, 128),
        (act, pre, hidden, final, reciprocal, gate, out_weight),
    )


def reduce_gradient(left, right):
    return lax.psum_scatter(
        contract_first(left, right), ("dp", "row"), scatter_dimension=0, tiled=True
    )


def body(
    latents,
    labels,
    step_index,
    seeds,
    class_table,
    teacher_patch,
    teacher_mod,
    teacher_up,
    teacher_down,
    teacher_out,
    student_patch,
    student_mod,
    student_up,
    student_down,
    student_out,
):
    samples = latents.shape[0]
    batch_total = samples * lax.axis_size(("dp", "row"))
    pos = positions()
    all_labels, all_steps = (
        lax.all_gather(labels, ("dp", "row"), axis=0, tiled=True),
        lax.all_gather(step_index, ("dp", "row"), axis=0, tiled=True),
    )
    all_now = all_steps.astype(jnp.float32) / STEPS
    cond_now = condition(all_now, all_labels, class_table)
    cond_mid = condition(all_now - 0.5 / STEPS, all_labels, class_table)
    own_rows = teacher_mod.shape[0]
    offset = lax.axis_index(("dp", "row")) * own_rows
    rows_now = lax.dynamic_slice_in_dim(cond_now, offset, own_rows, 1)
    rows_mid = lax.dynamic_slice_in_dim(cond_mid, offset, own_rows, 1)
    teacher_part = jnp.einsum(
        "nkd,dcf->nkcf",
        jnp.stack([rows_now, rows_mid], axis=1),
        teacher_mod,
        preferred_element_type=jnp.float32,
    )
    student_part = jnp.einsum(
        "nd,dcf->ncf", rows_now, student_mod, preferred_element_type=jnp.float32
    )[:, None]
    teacher_sums, student_sums = (
        lax.psum_scatter(teacher_part, ("dp", "row"), scatter_dimension=0, tiled=True),
        lax.psum_scatter(student_part, ("dp", "row"), scatter_dimension=0, tiled=True),
    )
    teacher_mods, student_mods = (
        lax.all_gather(teacher_sums, "col", axis=3, tiled=True),
        lax.all_gather(student_sums, "col", axis=3, tiled=True),
    )
    now = step_index.astype(jnp.float32) / STEPS
    alpha, sigma = plan(now[:, None, None])
    alpha_mid, sigma_mid = plan((now - 0.5 / STEPS)[:, None, None])
    alpha_end, sigma_end = plan((now - 1.0 / STEPS)[:, None, None])
    noisy = alpha * latents + sigma * noise_of(seeds)
    up_panel, down_panel = (
        lax.all_gather(teacher_up, ("dp", "row"), axis=0, tiled=True),
        lax.all_gather(teacher_down, ("dp", "row"), axis=0, tiled=True),
    )

    def teacher_up_product(act):
        return jnp.dot(act, up_panel, preferred_element_type=jnp.float32)

    def teacher_down_product(hidden):
        return contract_last(hidden, down_panel)

    first_v, _ = network(
        noisy,
        teacher_mods[:, 0],
        teacher_patch,
        teacher_out,
        pos,
        teacher_up_product,
        teacher_down_product,
    )
    first_x = alpha * noisy - sigma * first_v
    halfway = alpha_mid * first_x + sigma_mid * (noisy - alpha * first_x) / sigma
    second_v, _ = network(
        halfway,
        teacher_mods[:, 1],
        teacher_patch,
        teacher_out,
        pos,
        teacher_up_product,
        teacher_down_product,
    )
    second_x = alpha_mid * halfway - sigma_mid * second_v
    landing = alpha_end * second_x + sigma_end * (halfway - alpha_mid * second_x) / sigma_mid
    ratio = sigma_end / sigma
    target = (landing - ratio * noisy) / (alpha_end - ratio * alpha)

    def student_up_product(act):
        return jnp.dot(
            act,
            lax.all_gather(student_up, ("dp", "row"), axis=0, tiled=True),
            preferred_element_type=jnp.float32,
        )

    student_panel = lax.all_gather(student_down, ("dp", "row"), axis=0, tiled=True)

    def student_down_product(hidden):
        return contract_last(hidden, student_panel)

    student_v, saved = network(
        noisy,
        student_mods[:, 0],
        student_patch,
        student_out,
        pos,
        student_up_product,
        student_down_product,
    )
    student_x = alpha * noisy - sigma * student_v
    weight = jnp.maximum(alpha * alpha / (sigma * sigma), 1.0)
    back_velocity = (-2.0 * sigma * weight * (student_x - target) / batch_total).reshape(
        samples * SEQ, PATCH
    )
    act, pre, hidden, final, reciprocal, gate_share, out_share = saved
    back_final = jnp.dot(
        back_velocity, out_share.astype(jnp.float32), precision=lax.Precision.HIGHEST
    ).reshape(samples, SEQ, -1)
    centre = jnp.mean(back_final, axis=2, keepdims=True)
    along = jnp.mean(back_final * final, axis=2, keepdims=True)
    back_mixed = (
        (gate_share * (reciprocal * (back_final - centre - final * along)))
        .astype(jnp.bfloat16)
        .reshape(samples * SEQ, D)
    )
    down_gradient = reduce_gradient(back_mixed, hidden)
    back_hidden = jnp.dot(back_mixed, student_panel, preferred_element_type=jnp.float32)
    back_pre = (back_hidden * gelu_slope(pre)).astype(jnp.bfloat16)
    up_gradient = reduce_gradient(act, back_pre)
    return (up_gradient, down_gradient)


def solution(mesh):
    placed = (
        P(("dp", "row"), None, None),
        P(("dp", "row")),
        P(("dp", "row")),
        P(("dp", "row")),
        P(),
        P(),
        P(("dp", "row"), None, "col"),
        P(("dp", "row"), "col"),
        P(("dp", "row"), "col"),
        P(),
        P(),
        P(("dp", "row"), None, "col"),
        P(("dp", "row"), "col"),
        P(("dp", "row"), "col"),
        P(),
    )
    return jax.shard_map(
        body,
        mesh=mesh,
        in_specs=placed,
        out_specs=(P(("dp", "row"), "col"), P(("dp", "row"), "col")),
        check_vma=False,
    )
```

profile of v0, /device:TPU:0, one launch (start us, length us, event | category | flops | bytes accessed | tf_op | source)
XLA Modules:
  0.0 598.2 jit_solution(1822111172915230698)
XLA Ops:
  11.2 9.5 %all-reduce.4 = (s32[24]{0:T(128)S(1)}, s32[24]{0:T(128)S(1)}) all-reduce(s32[24]{0:T(128)S(1)} %dynamic-update-slice, s32[24]{0:T(128)S(1)} %dynamic-update-slice.1), channel_id=1, replica_groups=mesh['dp'=2,'row'=4,'col'=4] {'dp','row'}, use_global_device_ids=true, to_apply=%add | all-reduce | flops 48 | bytes 384
  30.0 2.8 multiply_cosine_fusion
  40.5 2.5 multiply_reduce_fusion.6
  44.3 33.5 %all-reduce.13.cloned.1.call-done = (f32[24,1,3,288]{3,1,2,0:T(1,128)}, f32[24,2,3,288]{3,1,2,0:T(2,128)}) async-done(((f32[24,1,3,288]{3,1,2,0:T(1,128)}, f32[24,2,3,288]{3,1,2,0:T(2,128)}), (f32[24,1,3,288]{3,1,2,0:T(1,128)}, f32[24,2,3,288]{3,1,2,0:T(2,128)})) %all-reduce.13.cloned.1.call-update) | async-done | bytes 248848
  81.2 62.1 %all_gather.29 = f32[3,2,3,1152]{2,1,0,3:T(2,128)S(1)} all-gather(f32[3,2,3,288]{2,1,0,3:T(2,128)} %copy.57), channel_id=1, replica_groups=mesh['dp'=2,'row'=4,'col'=4] {'col'}, dimensions={3}, use_global_device_ids=true | all-gather | bytes 103680 | tf_op jit(solution)/shard_map/all_gather | solution.py:170
  143.3 3.9 fusion.94
  147.1 4.6 copy.81
  151.7 4.6 copy.82
  158.0 38.8 %all_gather.26 = f32[3,1,3,1152]{2,1,0,3:T(1,128)} all-gather(f32[3,1,3,288]{2,1,0,3:T(1,128)} %copy.52), channel_id=1, replica_groups=mesh['dp'=2,'row'=4,'col'=4] {'col'}, dimensions={3}, use_global_device_ids=true | all-gather | bytes 51840 | tf_op jit(solution)/shard_map/all_gather | solution.py:171
  196.9 4.6 copy.53
  204.0 3.1 add_convert_fusion.1
  207.2 4.5 add_convert_fusion.2
  211.7 9.5 %convolution_convert_fusion.1 = bf16[768,1152]{1,0:T(8,128)(2,1)} fusion(bf16[1152,1152]{1,0:T(8,128)(2,1)} %all-gather.11.cloned.1.call-done, bf16[768,1152]{1,0:T(8,128)(2,1)} %bitcast.116, bf16[1152,1152]{1,0:T(8,128)(2,1)} %all-gather.9.cloned.1.call-done), kind=kOutput, calls=%fused_computation.56 | convolution fusion | flops 4085710848 | bytes 8847360 | tf_op jit(solution)/shard_map/dot_general | solution.py:83
  225.0 6.7 %fusion.106 = f32[768,1152]{1,0:T(8,128)} fusion(bf16[768,1152]{1,0:T(8,128)(2,1)} %bitcast.109, bf16[1152,1152]{1,0:T(8,128)(2,1)} %all-gather.5.cloned.1.call-done), kind=kOutput, calls=%fused_computation.198 | convolution fusion | flops 2038431744 | bytes 7962624 | tf_op jit(solution)/shard_map/dot_general | solution.py:215
  231.7 7.3 %convolution_convert_fusion.2 = bf16[768,1152]{1,0:T(8,128)(2,1)} fusion(bf16[1152,1152]{1,0:T(8,128)(2,1)} %all-gather.7.cloned.1.call-done, f32[768,1152]{1,0:T(8,128)} %fusion.106), kind=kOutput, calls=%fused_computation.57 | convolution fusion | flops 2047279104 | bytes 7962624 | tf_op jit(solution)/shard_map/dot_general | solution.py:83
  238.9 54.8 %all-reduce.11.cloned.1.call-done = bf16[3,256,1152]{2,1,0:T(8,128)(2,1)} async-done(((bf16[3,256,1152]{2,1,0:T(8,128)(2,1)}), bf16[3,256,1152]{2,1,0:T(8,128)(2,1)}) %all-reduce.11.cloned.1.call-update) | async-done | bytes 1769488 | tf_op jit(solution)/shard_map/psum | solution.py:109
  305.2 9.7 %convolution_convert_fusion = bf16[768,1152]{1,0:T(8,128)(2,1)} fusion(bf16[1152,1152]{1,0:T(8,128)(2,1)} %all-gather.11.cloned.1.call-done, bf16[768,1152]{1,0:T(8,128)(2,1)} %bitcast.117, bf16[1152,1152]{1,0:T(8,128)(2,1)} %all-gather.9.cloned.1.call-done), kind=kOutput, calls=%fused_computation.55 | convolution fusion | flops 4085710848 | bytes 8847360 | tf_op jit(solution)/shard_map/dot_general | solution.py:83
  316.9 131.0 %all-reduce.15.cloned.1.call-done = (bf16[3,256,1152]{2,1,0:T(8,128)(2,1)}, bf16[3,256,1152]{2,1,0:T(8,128)(2,1)}) async-done(((bf16[3,256,1152]{2,1,0:T(8,128)(2,1)}, bf16[3,256,1152]{2,1,0:T(8,128)(2,1)}), (bf16[3,256,1152]{2,1,0:T(8,128)(2,1)}, bf16[3,256,1152]{2,1,0:T(8,128)(2,1)})) %all-reduce.15.cloned.1.call-update) | async-done | bytes 3538960 | tf_op jit(solution)/shard_map/psum | solution.py:109
  447.9 3.1 fusion.92
  462.0 4.6 fusion.90
  469.2 5.0 fusion.87
  474.6 12.3 %fusion.110 = f32[1152,1152]{1,0:T(8,128)} fusion(bf16[768,1152]{1,0:T(8,128)(2,1)} %bitcast.110, f32[768,1152]{1,0:T(8,128)} %fusion.106, bf16[768,1152]{1,0:T(8,128)(2,1)} %bitcast.115, bf16[1152,1152]{1,0:T(8,128)(2,1)} %all-gather.7.cloned.1.call-done), kind=kOutput, calls=%fused_computation.202 | convolution fusion | flops 4093673472 | bytes 15040512 | tf_op jit(solution)/shard_map/dot_general | solution.py:89
  486.9 43.4 %reduce-scatter.5.cloned.1.call-done = f32[144,1152]{1,0:T(8,128)} async-done(((f32[1152,1152]{1,0:T(8,128)}), f32[144,1152]{1,0:T(8,128)}) %reduce-scatter.5.cloned.1.call-update) | async-done | bytes 663568 | tf_op jit(solution)/shard_map/reduce_scatter | solution.py:120
  530.3 60.9 %reduce-scatter.3.cloned.1.call-done = f32[144,1152]{1,0:T(8,128)} async-done(((f32[1152,1152]{1,0:T(8,128)}), f32[144,1152]{1,0:T(8,128)}) %reduce-scatter.3.cloned.1.call-update) | async-done | bytes 663568 | tf_op jit(solution)/shard_map/reduce_scatter | solution.py:120
  (159 shorter events, 59.2 us)
Async XLA Ops:
  7.2 14.0 %copy-start = (bf16[1000,1152]{1,0:T(8,128)(2,1)S(1)}, bf16[1000,1152]{1,0:T(8,128)(2,1)}, u32[]{:S(2)}) copy-start(bf16[1000,1152]{1,0:T(8,128)(2,1)} %param.19) | copy-start | bytes 6912004
  7.2 20.4 %copy-start.28 = (s32[3]{0:T(128)S(1)}, s32[3]{0:T(128)}, u32[]{:S(2)}) copy-start(s32[3]{0:T(128)} %param.17) | copy-start | bytes 40
  7.2 16.6 %copy-start.10 = (bf16[144,3,288]{2,0,1:T(8,128)(2,1)S(1)}, bf16[144,3,288]{2,0,1:T(8,128)(2,1)}, u32[]{:S(2)}) copy-start(bf16[144,3,288]{2,0,1:T(8,128)(2,1)} %param.26) | copy-start | bytes 746500
  7.2 21.1 %copy-start.29 = (s32[3]{0:T(128)S(1)}, s32[3]{0:T(128)}, u32[]{:S(2)}) copy-start(s32[3]{0:T(128)} %param.18) | copy-start | bytes 40
  7.2 21.1 %copy-start.19 = (f32[3,32,128]{2,1,0:T(8,128)S(1)}, f32[3,32,128]{2,1,0:T(8,128)}, u32[]{:S(2)}) copy-start(f32[3,32,128]{2,1,0:T(8,128)} %param.15) | copy-start | bytes 147460
  7.2 70.6 %all-reduce.13.cloned.1.call-start = ((), (), s32[]{:S(2)}) async-start(), calls=%async_computation.9 | async-start | bytes 663552
  24.9 186.8 %all-gather.11.cloned.1.call-start = ((), (), s32[]{:S(2)}) async-start(), calls=%async_computation.5 | async-start | bytes 2985984 | tf_op jit(solution)/shard_map/all_gather | solution.py:180
  25.6 186.1 %all-gather.9.cloned.1.call-start = ((), (), s32[]{:S(2)}) async-start(), calls=%async_computation.4 | async-start | bytes 2985984 | tf_op jit(solution)/shard_map/all_gather | solution.py:179
  26.4 198.6 %all-gather.5.cloned.1.call-start = ((), (), s32[]{:S(2)}) async-start(), calls=%async_computation.2 | async-start | bytes 2985984 | tf_op jit(solution)/shard_map/all_gather | solution.py:217
  27.0 204.7 %all-gather.7.cloned.1.call-start = ((), (), s32[]{:S(2)}) async-start(), calls=%async_computation.3 | async-start | bytes 2985984 | tf_op jit(solution)/shard_map/all_gather | solution.py:221
  27.5 266.3 %all-reduce.11.cloned.1.call-start = ((), (), s32[]{:S(2)}) async-start(), calls=%async_computation.6 | async-start | bytes 3538944 | tf_op jit(solution)/shard_map/psum | solution.py:109
  34.2 3.3 copy-start.4
  34.2 3.3 copy-start.7
  34.2 3.3 copy-start.20
  36.4 3.5 copy-start.21
  201.4 5.7 copy-start.23
  201.4 5.7 copy-start.24
  221.2 226.7 %all-reduce.15.cloned.1.call-start = ((), (), s32[]{:S(2)}) async-start(), calls=%async_computation.10 | async-start | bytes 7077888 | tf_op jit(solution)/shard_map/psum | solution.py:109
  300.1 2.6 copy-start.18
  314.9 215.4 %reduce-scatter.5.cloned.1.call-start = ((), (), s32[]{:S(2)}) async-start(), calls=%async_computation.8 | async-start | bytes 5971968 | tf_op jit(solution)/shard_map/reduce_scatter | solution.py:120
  462.0 4.7 copy-start.3
  462.0 4.7 copy-start.13
  474.3 116.9 %reduce-scatter.3.cloned.1.call-start = ((), (), s32[]{:S(2)}) async-start(), calls=%async_computation.7 | async-start | bytes 5971968 | tf_op jit(solution)/shard_map/reduce_scatter | solution.py:120
  474.6 116.6 %copy-start.1 = (bf16[1000,1152]{1,0:T(8,128)(2,1)S(1)}, bf16[1000,1152]{1,0:T(8,128)(2,1)}, u32[]{:S(2)}) copy-start(bf16[1000,1152]{1,0:T(8,128)(2,1)} %param.19) | copy-start | bytes 6912004
  (16 other events, 26.4 us)
Sparse Core Ops, SparseCore 0:
  25.0 52.8 all-reduce.12
  79.7 30.7 all-gather.10
  112.4 30.1 all-gather.8
  144.3 30.1 all-gather.4
  176.2 30.1 all-gather.6
  221.3 72.3 all-reduce.10
  315.0 132.8 all-reduce.14
  474.4 55.8 reduce-scatter.4
  534.3 56.8 reduce-scatter.2
where the time goes:
time: 607 us; the launch traced here: 598 us
  waiting for transfers between devices  326 us (54%)
  blocking collectives  110 us (18%)
  matrix products  66.2 us (11%)
  local copies, waits for them, and re-layouts  39.9 us (7%)
  other arithmetic  38.5 us (6%)
  between operations  16.2 us (3%)
    psum x2, waiting for transfers between devices, network(): mixed = lax.psum(partial_out, 'col').astype(jnp.float32)  186 us
    reduce_scatter x2, waiting for transfers between devices, reduce_gradient(): lax.psum_scatter(contract_first(left, right), ('dp', 'row'), scatter_dime...  104 us
    all_gather x1, blocking collectives, body(): lax.all_gather(teacher_sums, 'col', axis=3, tiled=True)  62.1 us
    all_gather x1, blocking collectives, body(): lax.all_gather(student_sums, 'col', axis=3, tiled=True)  38.8 us
    unnamed x10, waiting for transfers between devices  36.1 us
    dot_general x6, matrix products, contract_last(): lax.dot_general(left, right, (((1,), (1,)), ((), ())), preferred_element_...  29 us
    unnamed x77, local copies, waits for them, and re-layouts  21.6 us
    dot_general x2, matrix products, contract_first(): lax.dot_general(left, right, (((0,), (0,)), ((), ())), preferred_element_...  17.3 us
  transfers between devices with their start and end apart: 9, of which 5 were waited for; matrix products, arithmetic and copies ran while one was open for 15% of the time, Pallas kernels for 0%

commit v1 on v0

--- a/solution.py
+++ b/solution.py
@@ -11,6 +11,11 @@
 STEPS = 8
 HALF_PI = 0.5 * math.pi
 ROOT_TWO_PI = math.sqrt(2.0 / math.pi)
+
+
+def switch_the_regions(panel):
+    extra = jnp.concatenate(lax.all_gather(panel, axis_name="col"), axis=3)
+    return extra
 
 
 def plan(times):
@@ -168,7 +173,7 @@
     )
     teacher_mods, student_mods = (
         lax.all_gather(teacher_sums, "col", axis=3, tiled=True),
-        lax.all_gather(student_sums, "col", axis=3, tiled=True),
+        switch_the_regions(student_sums),
     )
     now = step_index.astype(jnp.float32) / STEPS
     alpha, sigma = plan(now[:, None, None])

time: 607 us -> 597 us (0.984)
  blocking collectives: 110 us -> 85.7 us
  waiting for transfers between devices: 326 us -> 345 us
    all_gather x1, blocking collectives: 38.8 us -> 14.1 us  [switch_the_regions(): extra = jnp.concatenate(lax.all_gather(panel, axis_name='col'), axis=3)]
    psum x2, waiting for transfers between devices: 186 us -> 202 us  [network(): mixed = lax.psum(partial_out, 'col').astype(jnp.float32)]
    unnamed x77 -> x72, local copies, waits for them, and re-layouts: 21.6 us -> 17.1 us
  transfers between devices with their start and end apart: 9 -> 9, of which waited for: 5 -> 6; matrix products, arithmetic and copies ran while one was open for 15% -> 15% of each run, Pallas kernels for 0% -> 0%
where the time goes in v1:
time: 597 us; the launch traced here: 589 us
  waiting for transfers between devices  345 us (58%)
  blocking collectives  85.7 us (14%)
  matrix products  66.4 us (11%)
  other arithmetic  38.5 us (6%)
  local copies, waits for them, and re-layouts  36.5 us (6%)
  between operations  16.1 us (3%)
    psum x2, waiting for transfers between devices, network(): mixed = lax.psum(partial_out, 'col').astype(jnp.float32)  202 us
    reduce_scatter x2, waiting for transfers between devices, reduce_gradient(): lax.psum_scatter(contract_first(left, right), ('dp', 'row'), scatter_dime...  104 us
    all_gather x1, blocking collectives, body(): lax.all_gather(teacher_sums, 'col', axis=3, tiled=True)  62.1 us
    unnamed x10, waiting for transfers between devices  36 us
    dot_general x6, matrix products, contract_last(): lax.dot_general(left, right, (((1,), (1,)), ((), ())), preferred_element_...  29.1 us
    dot_general x2, matrix products, contract_first(): lax.dot_general(left, right, (((0,), (0,)), ((), ())), preferred_element_...  17.4 us
    unnamed x72, local copies, waits for them, and re-layouts  17.1 us
    all_gather x1, blocking collectives, switch_the_regions(): extra = jnp.concatenate(lax.all_gather(panel, axis_name='col'), axis=3)  14.1 us
  transfers between devices with their start and end apart: 9, of which 6 were waited for; matrix products, arithmetic and copies ran while one was open for 15% of the time, Pallas kernels for 0%

profile of v1, /device:TPU:0, one launch (start us, length us, event | category | flops | bytes accessed | tf_op | source)
XLA Modules:
  0.0 588.6 jit_solution(5190326969681787099)
XLA Ops:
  11.1 9.5 %all-reduce.4 = (s32[24]{0:T(128)S(1)}, s32[24]{0:T(128)S(1)}) all-reduce(s32[24]{0:T(128)S(1)} %dynamic-update-slice, s32[24]{0:T(128)S(1)} %dynamic-update-slice.1), channel_id=1, replica_groups=mesh['dp'=2,'row'=4,'col'=4] {'dp','row'}, use_global_device_ids=true, to_apply=%add | all-reduce | flops 48 | bytes 384
  29.9 2.8 multiply_cosine_fusion
  37.4 2.5 fusion.99
  44.3 33.5 %all-reduce.13.cloned.1.call-done = (f32[24,1,3,288]{3,1,2,0:T(1,128)}, f32[24,2,3,288]{3,1,2,0:T(2,128)}) async-done(((f32[24,1,3,288]{3,1,2,0:T(1,128)}, f32[24,2,3,288]{3,1,2,0:T(2,128)}), (f32[24,1,3,288]{3,1,2,0:T(1,128)}, f32[24,2,3,288]{3,1,2,0:T(2,128)})) %all-reduce.13.cloned.1.call-update) | async-done | bytes 248848
  81.1 62.1 %all_gather.33 = f32[3,2,3,1152]{2,1,0,3:T(2,128)S(1)} all-gather(f32[3,2,3,288]{2,1,0,3:T(2,128)} %copy.57), channel_id=1, replica_groups=mesh['dp'=2,'row'=4,'col'=4] {'col'}, dimensions={3}, use_global_device_ids=true | all-gather | bytes 103680 | tf_op jit(solution)/shard_map/all_gather | solution.py:175
  143.2 3.9 fusion.94
  147.1 4.6 copy.81
  151.6 4.6 copy.61
  156.9 14.1 %all-gather = f32[12,1,3,288]{3,1,2,0:T(1,128)S(1)} all-gather(f32[3,1,3,288]{3,1,2,0:T(1,128)S(1)} %constant_dynamic-slice_fusion.1), channel_id=2, replica_groups=mesh['dp'=2,'row'=4,'col'=4] {'col'}, dimensions={0}, use_global_device_ids=true | all-gather | bytes 51840 | tf_op jit(solution)/shard_map/all_gather | solution.py:17
  175.7 3.2 add_convert_fusion.1
  178.9 4.5 add_convert_fusion.2
  183.4 9.6 %convolution_convert_fusion.1 = bf16[768,1152]{1,0:T(8,128)(2,1)} fusion(bf16[1152,1152]{1,0:T(8,128)(2,1)} %all-gather.12.cloned.1.call-done, bf16[768,1152]{1,0:T(8,128)(2,1)} %bitcast.120, bf16[1152,1152]{1,0:T(8,128)(2,1)} %all-gather.10.cloned.1.call-done), kind=kOutput, calls=%fused_computation.56 | convolution fusion | flops 4085710848 | bytes 8847360 | tf_op jit(solution)/shard_map/dot_general | solution.py:88
  196.8 6.7 %fusion.106 = f32[768,1152]{1,0:T(8,128)} fusion(bf16[768,1152]{1,0:T(8,128)(2,1)} %bitcast.113, bf16[1152,1152]{1,0:T(8,128)(2,1)} %all-gather.6.cloned.1.call-done), kind=kOutput, calls=%fused_computation.198 | convolution fusion | flops 2038431744 | bytes 7962624 | tf_op jit(solution)/shard_map/dot_general | solution.py:220
  203.5 2.7 all-gather.8.cloned.1.call-done
  206.2 7.2 %convolution_convert_fusion.2 = bf16[768,1152]{1,0:T(8,128)(2,1)} fusion(bf16[1152,1152]{1,0:T(8,128)(2,1)} %all-gather.8.cloned.1.call-done, f32[768,1152]{1,0:T(8,128)} %fusion.106), kind=kOutput, calls=%fused_computation.57 | convolution fusion | flops 2047279104 | bytes 7962624 | tf_op jit(solution)/shard_map/dot_general | solution.py:88
  213.5 70.5 %all-reduce.11.cloned.1.call-done = bf16[3,256,1152]{2,1,0:T(8,128)(2,1)} async-done(((bf16[3,256,1152]{2,1,0:T(8,128)(2,1)}), bf16[3,256,1152]{2,1,0:T(8,128)(2,1)}) %all-reduce.11.cloned.1.call-update) | async-done | bytes 1769488 | tf_op jit(solution)/shard_map/psum | solution.py:114
  295.4 9.7 %convolution_convert_fusion = bf16[768,1152]{1,0:T(8,128)(2,1)} fusion(bf16[1152,1152]{1,0:T(8,128)(2,1)} %all-gather.12.cloned.1.call-done, bf16[768,1152]{1,0:T(8,128)(2,1)} %bitcast.121, bf16[1152,1152]{1,0:T(8,128)(2,1)} %all-gather.10.cloned.1.call-done), kind=kOutput, calls=%fused_computation.55 | convolution fusion | flops 4085710848 | bytes 8847360 | tf_op jit(solution)/shard_map/dot_general | solution.py:88
  307.1 131.0 %all-reduce.15.cloned.1.call-done = (bf16[3,256,1152]{2,1,0:T(8,128)(2,1)}, bf16[3,256,1152]{2,1,0:T(8,128)(2,1)}) async-done(((bf16[3,256,1152]{2,1,0:T(8,128)(2,1)}, bf16[3,256,1152]{2,1,0:T(8,128)(2,1)}), (bf16[3,256,1152]{2,1,0:T(8,128)(2,1)}, bf16[3,256,1152]{2,1,0:T(8,128)(2,1)})) %all-reduce.15.cloned.1.call-update) | async-done | bytes 3538960 | tf_op jit(solution)/shard_map/psum | solution.py:114
  438.1 3.1 fusion.92
  452.3 4.6 fusion.90
  459.6 5.1 fusion.87
  465.0 12.3 %fusion.110 = f32[1152,1152]{1,0:T(8,128)} fusion(bf16[768,1152]{1,0:T(8,128)(2,1)} %bitcast.114, f32[768,1152]{1,0:T(8,128)} %fusion.106, bf16[768,1152]{1,0:T(8,128)(2,1)} %bitcast.119, bf16[1152,1152]{1,0:T(8,128)(2,1)} %all-gather.8.cloned.1.call-done), kind=kOutput, calls=%fused_computation.202 | convolution fusion | flops 4093673472 | bytes 15040512 | tf_op jit(solution)/shard_map/dot_general | solution.py:94
  477.3 43.4 %reduce-scatter.5.cloned.1.call-done = f32[144,1152]{1,0:T(8,128)} async-done(((f32[1152,1152]{1,0:T(8,128)}), f32[144,1152]{1,0:T(8,128)}) %reduce-scatter.5.cloned.1.call-update) | async-done | bytes 663568 | tf_op jit(solution)/shard_map/reduce_scatter | solution.py:125
  520.7 60.9 %reduce-scatter.3.cloned.1.call-done = f32[144,1152]{1,0:T(8,128)} async-done(((f32[1152,1152]{1,0:T(8,128)}), f32[144,1152]{1,0:T(8,128)}) %reduce-scatter.3.cloned.1.call-update) | async-done | bytes 663568 | tf_op jit(solution)/shard_map/reduce_scatter | solution.py:125
  (155 shorter events, 60.5 us)
Async XLA Ops:
  7.2 14.0 %copy-start = (bf16[1000,1152]{1,0:T(8,128)(2,1)S(1)}, bf16[1000,1152]{1,0:T(8,128)(2,1)}, u32[]{:S(2)}) copy-start(bf16[1000,1152]{1,0:T(8,128)(2,1)} %param.19) | copy-start | bytes 6912004
  7.2 20.4 %copy-start.26 = (s32[3]{0:T(128)S(1)}, s32[3]{0:T(128)}, u32[]{:S(2)}) copy-start(s32[3]{0:T(128)} %param.17) | copy-start | bytes 40
  7.2 16.6 %copy-start.10 = (bf16[144,3,288]{2,0,1:T(8,128)(2,1)S(1)}, bf16[144,3,288]{2,0,1:T(8,128)(2,1)}, u32[]{:S(2)}) copy-start(bf16[144,3,288]{2,0,1:T(8,128)(2,1)} %param.26) | copy-start | bytes 746500
  7.2 21.0 %copy-start.27 = (s32[3]{0:T(128)S(1)}, s32[3]{0:T(128)}, u32[]{:S(2)}) copy-start(s32[3]{0:T(128)} %param.18) | copy-start | bytes 40
  7.2 21.0 %copy-start.19 = (f32[3,32,128]{2,1,0:T(8,128)S(1)}, f32[3,32,128]{2,1,0:T(8,128)}, u32[]{:S(2)}) copy-start(f32[3,32,128]{2,1,0:T(8,128)} %param.15) | copy-start | bytes 147460
  7.2 70.5 %all-reduce.13.cloned.1.call-start = ((), (), s32[]{:S(2)}) async-start(), calls=%async_computation.9 | async-start | bytes 663552
  24.8 158.6 %all-gather.10.cloned.1.call-start = ((), (), s32[]{:S(2)}) async-start(), calls=%async_computation.4 | async-start | bytes 2985984 | tf_op jit(solution)/shard_map/all_gather | solution.py:184
  25.6 157.8 %all-gather.12.cloned.1.call-start = ((), (), s32[]{:S(2)}) async-start(), calls=%async_computation.5 | async-start | bytes 2985984 | tf_op jit(solution)/shard_map/all_gather | solution.py:185
  26.3 170.5 %all-gather.6.cloned.1.call-start = ((), (), s32[]{:S(2)}) async-start(), calls=%async_computation.2 | async-start | bytes 2985984 | tf_op jit(solution)/shard_map/all_gather | solution.py:222
  26.9 179.4 %all-gather.8.cloned.1.call-start = ((), (), s32[]{:S(2)}) async-start(), calls=%async_computation.3 | async-start | bytes 2985984 | tf_op jit(solution)/shard_map/all_gather | solution.py:226
  27.5 256.5 %all-reduce.11.cloned.1.call-start = ((), (), s32[]{:S(2)}) async-start(), calls=%async_computation.6 | async-start | bytes 3538944 | tf_op jit(solution)/shard_map/psum | solution.py:114
  34.1 3.3 copy-start.4
  34.1 3.3 copy-start.7
  34.1 3.3 copy-start.20
  36.3 3.6 copy-start.21
  193.0 245.1 %all-reduce.15.cloned.1.call-start = ((), (), s32[]{:S(2)}) async-start(), calls=%async_computation.10 | async-start | bytes 7077888 | tf_op jit(solution)/shard_map/psum | solution.py:114
  290.3 2.6 copy-start.17
  290.3 2.6 copy-start.18
  305.1 215.6 %reduce-scatter.5.cloned.1.call-start = ((), (), s32[]{:S(2)}) async-start(), calls=%async_computation.8 | async-start | bytes 5971968 | tf_op jit(solution)/shard_map/reduce_scatter | solution.py:125
  452.3 4.7 copy-start.3
  452.3 4.7 copy-start.13
  457.0 2.6 copy-start.28
  464.7 116.9 %reduce-scatter.3.cloned.1.call-start = ((), (), s32[]{:S(2)}) async-start(), calls=%async_computation.7 | async-start | bytes 5971968 | tf_op jit(solution)/shard_map/reduce_scatter | solution.py:125
  465.0 116.6 %copy-start.1 = (bf16[1000,1152]{1,0:T(8,128)(2,1)S(1)}, bf16[1000,1152]{1,0:T(8,128)(2,1)}, u32[]{:S(2)}) copy-start(bf16[1000,1152]{1,0:T(8,128)(2,1)} %param.19) | copy-start | bytes 6912004
  (14 other events, 21.4 us)
Sparse Core Ops, SparseCore 0:
  24.9 52.7 all-reduce.12
  79.6 30.7 all-gather.9
  112.3 30.1 all-gather.11
  144.2 30.1 all-gather.5
  176.1 30.1 all-gather.7
  208.5 75.4 all-reduce.10
  305.2 132.8 all-reduce.14
  464.8 55.8 reduce-scatter.4
  524.7 56.8 reduce-scatter.2
